TPU v7x, 128 devices: a whole 4x4x4 slice. The times are simulated.
128 devices in a mesh: env: 8 (over z, core), tm: 16 (over y, x).
Axes of the slice: x: 4, y: 4, z: 4, core: 2. Of those that a mesh axis runs over, the one named last changes fastest.
Arguments:
- observations: bfloat16 [16, 12288, 2048], P('env', 'tm'), may hold values from -6 to 6
- stored_values: float32 [16, 12288], P('env', 'tm'), may hold values from -3.6 to 3.6
- rewards: float32 [16, 12288], P('env', 'tm'), may hold values from -0.18 to 0.18
- episode_ends: int32 [16, 12288], P('env', 'tm'), may hold values 0 or 1
- stale_list: int32 [8, 16, 12], P('env', 'tm'), may hold values from -1 to 11, as said below
- discount_horizon: float32 [16], P('env'), may hold values from 10 to 98304
- trace_horizon: float32 [16], P('env'), may hold values from 10 to 98304
- bootstrap: float32 [16], P('env'), may hold values from -3.6 to 3.6
- norm_gain: float32 [2048], replicated, may hold values from 0.1 to 1.9
- input_weight: bfloat16 [2048, 4096], replicated, may hold values from -0.125 to 0.125
- value_head: bfloat16 [4096], replicated, may hold values from -0.09375 to 0.09375
Outputs:
- targets: float32 [16, 12288], P('env', 'tm')
- advantages: float32 [16, 12288], P('env', 'tm')
Inputs may be any that keep to these rules, and one draw needn't show every extreme that they name: `stale_list`: for each device (first two indices: env shard, time shard) the last dimension lists distinct local block numbers e * 6 + k (e an environment row within the env shard, k a block of 128 steps within the time shard), followed by -1 entries; on some device all 12 blocks are listed.
All inputs are finite; a program needn't handle non-finite values. No bound on the sum of `episode_ends` on one device may be relied on, other than what follows from the above.
Results may differ from a plain program's by a relative error of at most 0.0018.
Values may be sent and summed in bfloat16 or wider, within the bound.
A program may use at most 128 MiB of HBM per device.

v0:
```python
import functools

import jax
import jax.numpy as jnp
from jax import lax
from jax.experimental import pallas as pl
from jax.experimental.pallas import tpu as pltpu
from jax.sharding import PartitionSpec as P

BLOCK = 128
CHUNK = 512
PIECE = 32
FIELDS = 16
MESH = pl.DeviceIdType.MESH


def spread(pair, rows, half):
    row = lax.broadcasted_iota(jnp.int32, (rows, BLOCK), 0)
    return jnp.where(row < half, pair[0], pair[1])


def shifted_left(value, by):
    return pltpu.roll(value, value.shape[1] - by, 1)


def shifted_up(value, by):
    return pltpu.roll(value, value.shape[0] - by, 0)


def sweep_kernel(
    listed,
    discount_horizon,
    trace_horizon,
    bootstrap,
    obs,
    weight,
    stored,
    rewards,
    ends,
    gain,
    head,
    offset_ref,
    factor_ref,
    value_ref,
    message_ref,
    raw,
    held,
    normed_a,
    normed_b,
    fresh,
    packed,
    half_gain,
    head_rows,
    raw_sem,
    held_sem,
):
    slots, _, features = raw.shape
    width = held.shape[1]
    chunks = width // CHUNK
    env_rows, steps = stored.shape
    per_row = steps // BLOCK
    count = jnp.int32(0)
    for j in range(slots):
        count += (listed[0, 0, j] >= 0).astype(jnp.int32)
    groups = (count + 1) // 2

    def raw_copy(slot):
        block = jnp.maximum(listed[0, 0, slot], 0)
        return pltpu.make_async_copy(obs.at[block], raw.at[slot], raw_sem.at[slot])

    def held_copy(c):
        part = pl.ds(c * CHUNK, CHUNK)
        return pltpu.make_async_copy(
            weight.at[:, part], held.at[:, part], held_sem.at[c]
        )

    def start_raw(slot):
        @pl.when(slot < count)
        def _():
            raw_copy(slot).start()

    def wait_group(group):
        for side in range(2):
            slot = 2 * group + side

            @pl.when(slot < count)
            def _():
                raw_copy(slot).wait()

    def normalize(group, piece, target):
        per_block = BLOCK // PIECE
        slot = jnp.minimum(2 * group + piece // per_block, slots - 1)
        rows = pl.ds((piece % per_block) * PIECE, PIECE)
        widened = raw[slot, rows, :].astype(jnp.float32)
        square_mean = jnp.mean(widened * widened, axis=-1, keepdims=True)
        scaled = widened * lax.rsqrt(square_mean + 1e-05) * half_gain[...]
        target[pl.ds(piece * PIECE, PIECE), :] = scaled.astype(jnp.bfloat16)

    def run_group(group, source, target, may_be_first):
        pieces = 2 * BLOCK // PIECE
        total = jnp.zeros((2 * BLOCK, BLOCK), jnp.float32)
        for c in range(chunks):
            if may_be_first:

                @pl.when(group == 0)
                def _():
                    held_copy(c).wait()

            part = pl.ds(c * CHUNK, CHUNK)
            hidden = jnp.dot(
                source[...], held[:, part], preferred_element_type=jnp.float32
            )
            for k in range(CHUNK // BLOCK):
                here = hidden[:, k * BLOCK : (k + 1) * BLOCK]
                active = (here + here * jnp.tanh(here)).astype(jnp.bfloat16)
                line = c * (CHUNK // BLOCK) + k
                total += active.astype(jnp.float32) * head_rows[line : line + 1, :]
            for piece in range(c * pieces // chunks, (c + 1) * pieces // chunks):
                normalize(group + 1, piece, target)
        for side in range(2):
            slot = 2 * group + side
            scores = jnp.sum(
                total[side * BLOCK : (side + 1) * BLOCK].T, axis=0, keepdims=True
            )

            @pl.when(slot < count)
            def _():
                fresh[pl.ds(listed[0, 0, jnp.minimum(slot, slots - 1)], 1), :] = scores

    for e in range(env_rows):
        for k in range(per_row):
            row, part = pl.ds(e * per_row + k, 1), pl.ds(k * BLOCK, BLOCK)
            fresh[row, :] = stored[e : e + 1, part]
            packed[0, row, :] = rewards[e : e + 1, part]
            packed[1, row, :] = 1.0 - ends[e : e + 1, part].astype(jnp.float32)

    @pl.when(count > 0)
    def _():
        for slot in range(2):
            start_raw(slot)
        for c in range(chunks):
            held_copy(c).start()
            if c == chunks // 2:
                for slot in range(2, 4):
                    start_raw(slot)
        for slot in range(4, slots):
            start_raw(slot)
        half_gain[...] = 0.5 * gain[...]
        head_rows[...] = head[...].astype(jnp.float32)
        wait_group(0)
        for piece in range(2 * BLOCK // PIECE):
            normalize(0, piece, normed_a)

        def two_groups(i, carry):
            wait_group(2 * i + 1)
            run_group(2 * i, normed_a, normed_b, True)

            @pl.when(2 * i + 1 < groups)
            def _():
                wait_group(2 * i + 2)
                run_group(2 * i + 1, normed_b, normed_a, False)

            return carry

        lax.fori_loop(0, (groups + 1) // 2, two_groups, 0)

    rows = fresh.shape[0]
    half = per_row
    value = fresh[...]
    lane = lax.broadcasted_iota(jnp.int32, (rows, BLOCK), 1)
    row = lax.broadcasted_iota(jnp.int32, (rows, BLOCK), 0)
    place = jnp.where(row < half, row, row - half)
    discount = 1.0 - 1.0 / spread((discount_horizon[0], discount_horizon[1]), rows, half)
    trace = 1.0 - 1.0 / spread((trace_horizon[0], trace_horizon[1]), rows, half)
    live = row < env_rows * half
    reward = jnp.where(live, packed[0], 0.0)
    going = jnp.where(live, packed[1], 0.0)
    value = jnp.where(live, value, 0.0)
    turned = shifted_left(value, 1)
    following = jnp.where(lane < BLOCK - 1, turned, shifted_up(turned, 1))
    last = (lane == BLOCK - 1) & (place == half - 1)
    following = jnp.where(last, value, following)
    factor = discount * trace * going
    offset = reward + discount * going * following - value
    by = 1
    while by < BLOCK:
        inside = lane < BLOCK - by
        offset = offset + factor * jnp.where(inside, shifted_left(offset, by), 0.0)
        factor = factor * jnp.where(inside, shifted_left(factor, by), 1.0)
        by *= 2
    row_factor = jnp.broadcast_to(factor[:, :1], (rows, BLOCK))
    row_offset = jnp.broadcast_to(offset[:, :1], (rows, BLOCK))
    by = 1
    while by < half:
        inside = place + by < half
        row_offset = row_offset + row_factor * jnp.where(
            inside, shifted_up(row_offset, by), 0.0
        )
        row_factor = row_factor * jnp.where(inside, shifted_up(row_factor, by), 1.0)
        by *= 2
    inside = place + 1 < half
    offset = offset + factor * jnp.where(inside, shifted_up(row_offset, 1), 0.0)
    factor = factor * jnp.where(inside, shifted_up(row_factor, 1), 1.0)

    packed[0] = offset
    packed[1] = factor
    fresh[...] = value
    lanes = lax.broadcasted_iota(jnp.int32, (1, BLOCK), 1)
    line = jnp.zeros((1, BLOCK), jnp.float32)
    for e in range(env_rows):
        mine = live & (row >= e * half) & (row < (e + 1) * half)

        def mean_of(array):
            return jnp.sum(jnp.where(mine, array, 0.0), keepdims=True) / steps

        mean_offset, mean_factor = mean_of(offset), mean_of(factor)
        near, far = offset - mean_offset, factor - mean_factor
        items = (
            row_offset[e * half : e * half + 1, :1],
            row_factor[e * half : e * half + 1, :1],
            value[e * half : e * half + 1, :1],
            value[(e + 1) * half - 1 : (e + 1) * half, BLOCK - 1 :],
            mean_offset,
            mean_factor,
            mean_of(near * near),
            mean_of(near * far),
            mean_of(far * far),
            1.0 / trace[e * half : e * half + 1, :1],
            jnp.full((1, 1), bootstrap[e], jnp.float32),
        )
        for k, item in enumerate(items):
            line = jnp.where(lanes == e * FIELDS + k, item, line)
        for k in range(per_row):
            source, part = pl.ds(e * per_row + k, 1), pl.ds(k * BLOCK, BLOCK)
            offset_ref[e : e + 1, part] = packed[0, source, :]
            factor_ref[e : e + 1, part] = packed[1, source, :]
            value_ref[e : e + 1, part] = fresh[source, :]
    message_ref[...] = line.reshape(message_ref.shape)


def exchange_kernel(
    shards,
    message,
    offset_ref,
    factor_ref,
    value_ref,
    result,
    gathered,
    partial,
    joined,
    send_sem,
    recv_sem,
    partial_sem,
    joined_sem,
):
    env, tm = lax.axis_index("env"), lax.axis_index("tm")
    envs = joined.shape[0]
    barrier = pltpu.get_barrier_semaphore()

    def each_shard(act):
        def one(i, carry):
            act(env, (tm + shards // 2 + i) % shards)
            return carry

        lax.fori_loop(0, shards // 2, one, 0)
        lax.fori_loop(shards // 2 + 1, shards, one, 0)

    def each_env(act):
        def one(i, carry):
            act((env + envs // 2 + i) % envs, tm)
            return carry

        lax.fori_loop(0, envs // 2, one, 0)
        lax.fori_loop(envs // 2 + 1, envs, one, 0)

    def greet(to_env, to_tm):
        pl.semaphore_signal(
            barrier, inc=1, device_id=(to_env, to_tm), device_id_type=MESH
        )

    def send(source, target, own, start_sem, end_sem):
        def act(to_env, to_tm):
            pltpu.make_async_remote_copy(
                src_ref=source,
                dst_ref=target.at[pl.ds(own, 1)],
                send_sem=start_sem,
                recv_sem=end_sem,
                device_id=(to_env, to_tm),
                device_id_type=MESH,
            ).start()

        return act

    def settle(target, length, sem):
        part = target.at[pl.ds(0, length)]
        pltpu.make_async_copy(part, part, sem).wait()

    gathered[...] = jnp.zeros_like(gathered)
    each_shard(greet)
    each_env(greet)
    pl.semaphore_wait(barrier, shards + envs - 2)
    each_shard(send(message, gathered, tm, send_sem, recv_sem))
    gathered[pl.ds(tm, 1)] = message[...]
    settle(gathered, shards - 1, recv_sem)

    fields = gathered[...].reshape(BLOCK, BLOCK).T
    pair = lax.broadcasted_iota(jnp.int32, (8, BLOCK), 0)
    lane = lax.broadcasted_iota(jnp.int32, (8, BLOCK), 1)

    def field(k):
        first = jnp.broadcast_to(fields[k : k + 1], (8, BLOCK))
        second = jnp.broadcast_to(fields[FIELDS + k : FIELDS + k + 1], (8, BLOCK))
        return jnp.where(pair == 0, first, second)

    offset, factor, last = field(0), field(1), field(3)
    following = jnp.where(lane < shards - 1, shifted_left(field(2), 1), field(10))
    jump = (following - last) * field(9)
    reached = offset + factor * jump
    by = 1
    while by < shards:
        inside = lane + by < shards
        reached = reached + factor * jnp.where(inside, shifted_left(reached, by), 0.0)
        factor = factor * jnp.where(inside, shifted_left(factor, by), 1.0)
        by *= 2
    entering = jump + jnp.where(lane < shards - 1, shifted_left(reached, 1), 0.0)
    mean = field(4) + entering * field(5)
    inner = field(6) + entering * (2.0 * field(7) + entering * field(8))
    counted = (pair < 2) & (lane < shards)

    def over_rows(array):
        return jnp.sum(jnp.where(counted, array, 0.0), keepdims=True) / (2 * shards)

    env_mean = over_rows(mean)
    off = mean - env_mean
    env_var = over_rows(inner + off * off)
    place = lax.broadcasted_iota(jnp.int32, (1, BLOCK), 1)
    line = jnp.where(place == 0, env_mean, jnp.where(place == 1, env_var, 0.0))
    partial[...] = line.reshape(partial.shape)
    own = jnp.sum(jnp.where(lane == tm, entering, 0.0), axis=1, keepdims=True)
    advantage = offset_ref[...] + factor_ref[...] * own[:2]
    result[0] = advantage + value_ref[...]
    each_env(send(partial, joined, env, partial_sem, joined_sem))
    joined[pl.ds(env, 1)] = partial[...]
    settle(joined, envs - 1, joined_sem)

    both = joined[...].reshape(envs, BLOCK)
    means, spans = both[:, :1], both[:, 1:2]
    adv_mean = jnp.sum(means, keepdims=True) / envs
    away = means - adv_mean
    adv_var = jnp.sum(spans + away * away, keepdims=True) / envs
    result[1] = (advantage - adv_mean) * lax.rsqrt(adv_var + 1e-05)
    settle(gathered, shards - 1, send_sem)
    settle(joined, envs - 1, partial_sem)


def on_device(
    observations,
    stored_values,
    rewards,
    episode_ends,
    stale_list,
    discount_horizon,
    trace_horizon,
    bootstrap,
    norm_gain,
    input_weight,
    value_head,
):
    env_rows, steps, features = observations.shape
    slots = env_rows * steps // BLOCK
    width = input_weight.shape[1]
    shape = jax.ShapeDtypeStruct((env_rows, steps), jnp.float32)
    vmem, smem, anywhere = (
        pl.BlockSpec(memory_space=pltpu.VMEM),
        pl.BlockSpec(memory_space=pltpu.SMEM),
        pl.BlockSpec(memory_space=pltpu.HBM),
    )
    offset, factor, value, message = pl.pallas_call(
        sweep_kernel,
        name="sweep",
        out_shape=(shape, shape, shape, jax.ShapeDtypeStruct((1, 1, BLOCK), jnp.float32)),
        in_specs=[smem] * 4 + [anywhere] * 2 + [vmem] * 5,
        out_specs=[vmem] * 4,
        scratch_shapes=[
            pltpu.VMEM((slots, BLOCK, features), jnp.bfloat16),
            pltpu.VMEM((features, width), jnp.bfloat16),
            pltpu.VMEM((2 * BLOCK, features), jnp.bfloat16),
            pltpu.VMEM((2 * BLOCK, features), jnp.bfloat16),
            pltpu.VMEM((16, BLOCK), jnp.float32),
            pltpu.VMEM((2, 16, BLOCK), jnp.float32),
            pltpu.VMEM((1, features), jnp.float32),
            pltpu.VMEM((width // BLOCK, BLOCK), jnp.float32),
            pltpu.SemaphoreType.DMA((slots,)),
            pltpu.SemaphoreType.DMA((width // CHUNK,)),
        ],
        compiler_params=pltpu.CompilerParams(vmem_limit_bytes=59 * 1024 * 1024),
    )(
        stale_list,
        discount_horizon,
        trace_horizon,
        bootstrap,
        observations.reshape(slots, BLOCK, features),
        input_weight,
        stored_values,
        rewards,
        episode_ends,
        norm_gain.reshape(1, features),
        value_head.reshape(width // BLOCK, BLOCK),
    )
    envs, shards = lax.axis_size("env"), lax.axis_size("tm")
    joined = pl.pallas_call(
        functools.partial(exchange_kernel, shards),
        name="exchange",
        out_shape=jax.ShapeDtypeStruct((2, env_rows, steps), jnp.float32),
        in_specs=[vmem] * 4,
        out_specs=vmem,
        scratch_shapes=[
            pltpu.VMEM((BLOCK, 1, BLOCK), jnp.float32),
            pltpu.VMEM((1, 1, BLOCK), jnp.float32),
            pltpu.VMEM((envs, 1, BLOCK), jnp.float32),
        ]
        + [pltpu.SemaphoreType.DMA] * 4,
        compiler_params=pltpu.CompilerParams(
            collective_id=0, has_side_effects=True, vmem_limit_bytes=4 * 1024 * 1024
        ),
    )(message, offset, factor, value)
    return joined[0], joined[1]


def solution(mesh):
    placed = (
        P("env", "tm", None),
        P("env", "tm"),
        P("env", "tm"),
        P("env", "tm"),
        P("env", "tm", None),
        P("env"),
        P("env"),
        P("env"),
        P(),
        P(),
        P(),
    )
    return jax.shard_map(
        on_device,
        mesh=mesh,
        in_specs=placed,
        out_specs=(P("env", "tm"), P("env", "tm")),
        check_vma=False,
    )
```

profile of v0, /device:TPU:1, one launch (start us, length us, event | category | flops | bytes accessed | tf_op | source)
XLA Modules:
  0.0 58.5 jit_solution(4851250737585791420)
XLA Ops:
  0.6 34.6 %sweep.1 = (f32[2,768]{1,0:T(2,128)}, f32[2,768]{1,0:T(2,128)}, f32[2,768]{1,0:T(2,128)}, f32[1,1,128]{2,1,0:T(1,128)}) custom-call(s32[1,1,12]{2,1,0:T(1,128)} %listed.1, f32[2]{0:T(128)} %discount_horizon.1, f32[2]{0:T(128)} %trace_horizon.1, f32[2]{0:T(128)} %bootstrap.1, bf16[12,128,2048]{2,1,0:T(8,128)(2,1)} %bitcast.7, bf16[2048,4096]{1,0:T(8,128)(2,1)} %weight.1, ...), custom_call_target="tpu_custom_call" | custom-call | tf_op jit(solution)/shard_map/sweep/pallas_call | solution.py:378
  35.2 0.0 copy-start
  35.2 0.7 %copy-done = f32[2,768]{1,0:T(2,128)S(1)} copy-done((f32[2,768]{1,0:T(2,128)S(1)}, f32[2,768]{1,0:T(2,128)}, u32[]{:S(2)}) %copy-start) | copy-done | bytes 6168
  35.9 0.0 copy-start.1
  35.9 0.7 %copy-done.1 = f32[2,768]{1,0:T(2,128)S(1)} copy-done((f32[2,768]{1,0:T(2,128)S(1)}, f32[2,768]{1,0:T(2,128)}, u32[]{:S(2)}) %copy-start.1) | copy-done | bytes 6168
  36.6 0.0 copy-start.2
  36.6 0.7 %copy-done.2 = f32[2,768]{1,0:T(2,128)S(1)} copy-done((f32[2,768]{1,0:T(2,128)S(1)}, f32[2,768]{1,0:T(2,128)}, u32[]{:S(2)}) %copy-start.2) | copy-done | bytes 6168
  37.3 0.0 copy-start.3
  37.3 0.7 %copy-done.3 = f32[1,1,128]{2,1,0:T(1,128)S(1)} copy-done((f32[1,1,128]{2,1,0:T(1,128)S(1)}, f32[1,1,128]{2,1,0:T(1,128)}, u32[]{:S(2)}) %copy-start.3) | copy-done | bytes 536
  38.0 20.0 %exchange.1 = f32[2,2,768]{2,1,0:T(2,128)S(1)} custom-call(f32[1,1,128]{2,1,0:T(1,128)S(1)} %copy-done.3, f32[2,768]{1,0:T(2,128)S(1)} %copy-done, f32[2,768]{1,0:T(2,128)S(1)} %copy-done.1, f32[2,768]{1,0:T(2,128)S(1)} %copy-done.2), custom_call_target="tpu_custom_call" | custom-call | tf_op jit(solution)/shard_map/exchange/pallas_call | solution.py:411
  57.9 0.6 %slice_bitcast_fusion = (f32[2,768]{1,0:T(2,128)}, f32[2,768]{1,0:T(2,128)}) fusion(f32[2,2,768]{2,1,0:T(2,128)S(1)} %exchange.1), kind=kLoop, calls=%fused_computation | loop fusion | bytes 24576 | tf_op jit(solution)/shard_map/squeeze | solution.py:427
Async XLA Ops:
  35.2 0.7 %copy-start = (f32[2,768]{1,0:T(2,128)S(1)}, f32[2,768]{1,0:T(2,128)}, u32[]{:S(2)}) copy-start(f32[2,768]{1,0:T(2,128)} %get-tuple-element.7.offset_ref) | copy-start | bytes 18436
  35.9 0.7 %copy-start.1 = (f32[2,768]{1,0:T(2,128)S(1)}, f32[2,768]{1,0:T(2,128)}, u32[]{:S(2)}) copy-start(f32[2,768]{1,0:T(2,128)} %get-tuple-element.8.factor_ref) | copy-start | bytes 18436
  36.6 0.7 %copy-start.2 = (f32[2,768]{1,0:T(2,128)S(1)}, f32[2,768]{1,0:T(2,128)}, u32[]{:S(2)}) copy-start(f32[2,768]{1,0:T(2,128)} %get-tuple-element.9.value_ref) | copy-start | bytes 18436
  37.3 0.7 %copy-start.3 = (f32[1,1,128]{2,1,0:T(1,128)S(1)}, f32[1,1,128]{2,1,0:T(1,128)}, u32[]{:S(2)}) copy-start(f32[1,1,128]{2,1,0:T(1,128)} %get-tuple-element.6.message) | copy-start | bytes 1540
where the time goes:
time: 59.7 us; the launch traced here: 58.5 us
  Pallas kernels  54.5 us (91%)
  local copies, waits for them, and re-layouts  3.35 us (6%)
  between operations  0.66 us (1%)
    pallas_call x1, Pallas kernels, on_device(): pl.pallas_call(sweep_kernel, name='sweep', out_shape=(shape, shape, shape...  34.6 us
    pallas_call x1, Pallas kernels, on_device(): pl.pallas_call(functools.partial(exchange_kernel, shards), name='exchange...  20 us
    unnamed x8, local copies, waits for them, and re-layouts  2.75 us

commit v1 on v0

v1 whole, which is shorter than its diff:
```python
import functools

import jax
import jax.numpy as jnp
from jax import lax
from jax.experimental import pallas as pl
from jax.experimental.pallas import tpu as pltpu
from jax.sharding import PartitionSpec as P

BLOCK = 128
CHUNK = 512
PIECE = 32
FIELDS = 16
ROWS = 16
SWAP_LIMIT = 4 * 1024 * 1024
CRITIC_LIMIT = 36 * 1024 * 1024
EXCHANGE_LIMIT = 59 * 1024 * 1024
MESH = pl.DeviceIdType.MESH


def spread(pair, rows, half):
    row = lax.broadcasted_iota(jnp.int32, (rows, BLOCK), 0)
    return jnp.where(row < half, pair[0], pair[1])


def partner_of(env):
    return env + 1 - 2 * (env % 2)


def shifted_left(value, by):
    return pltpu.roll(value, value.shape[1] - by, 1)


def shifted_up(value, by):
    return pltpu.roll(value, value.shape[0] - by, 0)


def swap_kernel(
    obs, listed, weight, lent, their_list, held, send_sems, recv_sems, held_sems
):
    chunk = weight.shape[0] // held_sems.shape[0]
    loads = []
    for k in range(held_sems.shape[0]):
        part = pl.ds(k * chunk, chunk)
        loads.append(
            pltpu.make_async_copy(weight.at[part], held.at[part], held_sems.at[k])
        )
    env, tm = lax.axis_index("env"), lax.axis_index("tm")
    partner = partner_of(env)
    barrier = pltpu.get_barrier_semaphore()
    pl.semaphore_signal(barrier, inc=1, device_id=(partner, tm), device_id_type=MESH)
    pl.semaphore_wait(barrier, 1)
    pieces = lent.shape[0]
    kept = obs.shape[0] - pieces

    def remote(source, target, k):
        return pltpu.make_async_remote_copy(
            src_ref=source,
            dst_ref=target,
            send_sem=send_sems.at[k],
            recv_sem=recv_sems.at[k],
            device_id=(partner, tm),
            device_id_type=MESH,
        )

    copies = [remote(listed, their_list, pieces)]
    for k in range(pieces):
        copies.append(remote(obs.at[kept + k], lent.at[k], k))
    for copy in copies:
        copy.start()
    for load in loads:
        load.start()
    for load in loads:
        load.wait()
    for copy in copies:
        copy.wait()


def critic_kernel(
    listed,
    their_list,
    obs,
    lent,
    weight,
    stored,
    rewards,
    ends,
    gain,
    head,
    board,
    raw,
    normed_a,
    normed_b,
    half_gain,
    head_rows,
    flags,
    plan,
    raw_sem,
):
    slots, _, features = raw.shape
    chunks = weight.shape[1] // CHUNK
    env_rows, steps = stored.shape
    per_row = steps // BLOCK
    kept = slots - lent.shape[0]

    def read_list(source, own):
        for p in range(slots):
            flags[own, p] = 0
        total = jnp.int32(0)
        for j in range(slots):
            block = source[0, 0, j]
            total += (block >= 0).astype(jnp.int32)

            @pl.when(block >= 0)
            def _():
                flags[own, block] = 1

        movable = jnp.int32(0)
        for p in range(kept, slots):
            movable += flags[own, p]
        return total, movable

    mine, mine_movable = read_list(listed, 0)
    theirs, theirs_movable = read_list(their_list, 1)
    given = jnp.minimum(jnp.maximum((mine - theirs) // 2, 0), mine_movable)
    taken = jnp.minimum(jnp.maximum((theirs - mine) // 2, 0), theirs_movable)
    count = jnp.int32(0)
    for p in reversed(range(slots)):
        flag = flags[0, p]
        moves = flag * (given > 0).astype(jnp.int32)
        given -= moves
        plan[count] = p
        count += flag - moves
    for p in reversed(range(kept, slots)):
        moves = flags[1, p] * (taken > 0).astype(jnp.int32)
        taken -= moves
        plan[count] = ROWS + p
        count += moves
    groups = (count + 1) // 2

    def raw_copy(slot, act):
        entry = plan[slot]

        @pl.when((slot < count) & (entry < ROWS))
        def _():
            act(pltpu.make_async_copy(obs.at[entry], raw.at[slot], raw_sem.at[slot]))

        @pl.when((slot < count) & (entry >= ROWS))
        def _():
            block = entry - ROWS - kept
            act(pltpu.make_async_copy(lent.at[block], raw.at[slot], raw_sem.at[slot]))

    def wait_group(group):
        for side in range(2):
            raw_copy(2 * group + side, lambda copy: copy.wait())

    def normalize(group, piece, target):
        per_block = BLOCK // PIECE
        slot = jnp.minimum(2 * group + piece // per_block, slots - 1)
        rows = pl.ds((piece % per_block) * PIECE, PIECE)
        widened = raw[slot, rows, :].astype(jnp.float32)
        square_mean = jnp.mean(widened * widened, axis=-1, keepdims=True)
        scaled = widened * lax.rsqrt(square_mean + 1e-05) * half_gain[...]
        target[pl.ds(piece * PIECE, PIECE), :] = scaled.astype(jnp.bfloat16)

    def run_group(group, source, target):
        pieces = 2 * BLOCK // PIECE
        total = jnp.zeros((2 * BLOCK, BLOCK), jnp.float32)
        for c in range(chunks):
            part = pl.ds(c * CHUNK, CHUNK)
            hidden = jnp.dot(
                source[...], weight[:, part], preferred_element_type=jnp.float32
            )
            for k in range(CHUNK // BLOCK):
                here = hidden[:, k * BLOCK : (k + 1) * BLOCK]
                active = (here + here * jnp.tanh(here)).astype(jnp.bfloat16)
                line = c * (CHUNK // BLOCK) + k
                total += active.astype(jnp.float32) * head_rows[line : line + 1, :]
            for piece in range(c * pieces // chunks, (c + 1) * pieces // chunks):
                normalize(group + 1, piece, target)
        for side in range(2):
            slot = 2 * group + side
            scores = jnp.sum(
                total[side * BLOCK : (side + 1) * BLOCK].T, axis=0, keepdims=True
            )
            entry = plan[slot]

            @pl.when((slot < count) & (entry < ROWS))
            def _():
                board[0, pl.ds(entry, 1), :] = scores

            @pl.when((slot < count) & (entry >= ROWS))
            def _():
                board[3, pl.ds(entry - ROWS, 1), :] = scores

    for slot in range(slots):
        raw_copy(slot, lambda copy: copy.start())
    board[...] = jnp.zeros_like(board)
    for e in range(env_rows):
        for k in range(per_row):
            block, part = e * per_row + k, pl.ds(k * BLOCK, BLOCK)
            row = pl.ds(block, 1)
            board[0, row, :] = jnp.where(
                flags[0, block] > 0, 0.0, stored[e : e + 1, part]
            )
            board[1, row, :] = rewards[e : e + 1, part]
            board[2, row, :] = 1.0 - ends[e : e + 1, part].astype(jnp.float32)

    @pl.when(count > 0)
    def _():
        half_gain[...] = 0.5 * gain[...]
        head_rows[...] = head[...].astype(jnp.float32)
        wait_group(0)
        for piece in range(2 * BLOCK // PIECE):
            normalize(0, piece, normed_a)

        def two_groups(i, carry):
            wait_group(2 * i + 1)
            run_group(2 * i, normed_a, normed_b)

            @pl.when(2 * i + 1 < groups)
            def _():
                wait_group(2 * i + 2)
                run_group(2 * i + 1, normed_b, normed_a)

            return carry

        lax.fori_loop(0, (groups + 1) // 2, two_groups, 0)


def exchange_kernel(
    shards,
    discount_horizon,
    trace_horizon,
    bootstrap,
    board,
    result,
    held,
    returned,
    message,
    gathered,
    partial,
    joined,
    send_sem,
    recv_sem,
    partial_sem,
    joined_sem,
    board_sem,
    lend_sem,
    return_sem,
):
    env, tm = lax.axis_index("env"), lax.axis_index("tm")
    envs = joined.shape[0]
    barrier = pltpu.get_barrier_semaphore()

    def each_shard(act):
        def one(i, carry):
            act(env, (tm + shards // 2 + i) % shards)
            return carry

        lax.fori_loop(0, shards // 2, one, 0)
        lax.fori_loop(shards // 2 + 1, shards, one, 0)

    def each_env(act):
        def one(i, carry):
            act((env + envs // 2 + i) % envs, tm)
            return carry

        lax.fori_loop(0, envs // 2, one, 0)
        lax.fori_loop(envs // 2 + 1, envs, one, 0)

    def greet(to_env, to_tm):
        pl.semaphore_signal(
            barrier, inc=1, device_id=(to_env, to_tm), device_id_type=MESH
        )

    def send(source, target, own, start_sem, end_sem):
        def act(to_env, to_tm):
            pltpu.make_async_remote_copy(
                src_ref=source,
                dst_ref=target.at[pl.ds(own, 1)],
                send_sem=start_sem,
                recv_sem=end_sem,
                device_id=(to_env, to_tm),
                device_id_type=MESH,
            ).start()

        return act

    def settle(target, length, sem):
        part = target.at[pl.ds(0, length)]
        pltpu.make_async_copy(part, part, sem).wait()

    load = pltpu.make_async_copy(board, held, board_sem)
    load.start()
    gathered[...] = jnp.zeros_like(gathered)
    each_shard(greet)
    each_env(greet)
    pl.semaphore_wait(barrier, shards + envs - 2)
    load.wait()
    give_back = pltpu.make_async_remote_copy(
        src_ref=held.at[3],
        dst_ref=returned,
        send_sem=lend_sem,
        recv_sem=return_sem,
        device_id=(partner_of(env), tm),
        device_id_type=MESH,
    )
    give_back.start()
    give_back.wait()

    env_rows, steps = result.shape[1:]
    rows, half = ROWS, steps // BLOCK
    value = held[0] + returned[...]
    lane = lax.broadcasted_iota(jnp.int32, (rows, BLOCK), 1)
    row = lax.broadcasted_iota(jnp.int32, (rows, BLOCK), 0)
    place = jnp.where(row < half, row, row - half)
    discount = 1.0 - 1.0 / spread((discount_horizon[0], discount_horizon[1]), rows, half)
    trace = 1.0 - 1.0 / spread((trace_horizon[0], trace_horizon[1]), rows, half)
    live = row < env_rows * half
    reward = held[1]
    going = held[2]
    turned = shifted_left(value, 1)
    following = jnp.where(lane < BLOCK - 1, turned, shifted_up(turned, 1))
    last = (lane == BLOCK - 1) & (place == half - 1)
    following = jnp.where(last, value, following)
    factor = discount * trace * going
    offset = reward + discount * going * following - value
    by = 1
    while by < BLOCK:
        inside = lane < BLOCK - by
        offset = offset + factor * jnp.where(inside, shifted_left(offset, by), 0.0)
        factor = factor * jnp.where(inside, shifted_left(factor, by), 1.0)
        by *= 2
    row_factor = jnp.broadcast_to(factor[:, :1], (rows, BLOCK))
    row_offset = jnp.broadcast_to(offset[:, :1], (rows, BLOCK))
    by = 1
    while by < half:
        inside = place + by < half
        row_offset = row_offset + row_factor * jnp.where(
            inside, shifted_up(row_offset, by), 0.0
        )
        row_factor = row_factor * jnp.where(inside, shifted_up(row_factor, by), 1.0)
        by *= 2
    inside = place + 1 < half
    offset = offset + factor * jnp.where(inside, shifted_up(row_offset, 1), 0.0)
    factor = factor * jnp.where(inside, shifted_up(row_factor, 1), 1.0)
    lanes = lax.broadcasted_iota(jnp.int32, (1, BLOCK), 1)
    line = jnp.zeros((1, BLOCK), jnp.float32)
    for e in range(env_rows):
        mine = live & (row >= e * half) & (row < (e + 1) * half)

        def mean_of(array):
            return jnp.sum(jnp.where(mine, array, 0.0), keepdims=True) / steps

        mean_offset, mean_factor = mean_of(offset), mean_of(factor)
        near, far = offset - mean_offset, factor - mean_factor
        items = (
            row_offset[e * half : e * half + 1, :1],
            row_factor[e * half : e * half + 1, :1],
            value[e * half : e * half + 1, :1],
            value[(e + 1) * half - 1 : (e + 1) * half, BLOCK - 1 :],
            mean_offset,
            mean_factor,
            mean_of(near * near),
            mean_of(near * far),
            mean_of(far * far),
            1.0 / trace[e * half : e * half + 1, :1],
            jnp.full((1, 1), bootstrap[e], jnp.float32),
        )
        for k, item in enumerate(items):
            line = jnp.where(lanes == e * FIELDS + k, item, line)
    message[...] = line.reshape(message.shape)
    each_shard(send(message, gathered, tm, send_sem, recv_sem))
    gathered[pl.ds(tm, 1)] = message[...]
    settle(gathered, shards - 1, recv_sem)

    fields = gathered[...].reshape(BLOCK, BLOCK).T
    pair = lax.broadcasted_iota(jnp.int32, (8, BLOCK), 0)
    spot = lax.broadcasted_iota(jnp.int32, (8, BLOCK), 1)

    def field(k):
        first = jnp.broadcast_to(fields[k : k + 1], (8, BLOCK))
        second = jnp.broadcast_to(fields[FIELDS + k : FIELDS + k + 1], (8, BLOCK))
        return jnp.where(pair == 0, first, second)

    start, scale, end = field(0), field(1), field(3)
    following = jnp.where(spot < shards - 1, shifted_left(field(2), 1), field(10))
    jump = (following - end) * field(9)
    reached = start + scale * jump
    by = 1
    while by < shards:
        inside = spot + by < shards
        reached = reached + scale * jnp.where(inside, shifted_left(reached, by), 0.0)
        scale = scale * jnp.where(inside, shifted_left(scale, by), 1.0)
        by *= 2
    entering = jump + jnp.where(spot < shards - 1, shifted_left(reached, 1), 0.0)
    mean = field(4) + entering * field(5)
    inner = field(6) + entering * (2.0 * field(7) + entering * field(8))
    counted = (pair < 2) & (spot < shards)

    def over_rows(array):
        return jnp.sum(jnp.where(counted, array, 0.0), keepdims=True) / (2 * shards)

    env_mean = over_rows(mean)
    off = mean - env_mean
    env_var = over_rows(inner + off * off)
    place = lax.broadcasted_iota(jnp.int32, (1, BLOCK), 1)
    line = jnp.where(place == 0, env_mean, jnp.where(place == 1, env_var, 0.0))
    partial[...] = line.reshape(partial.shape)
    own = jnp.sum(jnp.where(spot == tm, entering, 0.0), axis=1, keepdims=True)
    advantage = offset + factor * jnp.where(row < half, own[:1], own[1:2])

    def put(which, array):
        for e in range(env_rows):
            for k in range(half):
                line = e * half + k
                result[which, e : e + 1, pl.ds(k * BLOCK, BLOCK)] = array[line : line + 1]

    put(0, advantage + value)
    each_env(send(partial, joined, env, partial_sem, joined_sem))
    joined[pl.ds(env, 1)] = partial[...]
    settle(joined, envs - 1, joined_sem)

    both = joined[...].reshape(envs, BLOCK)
    means, spans = both[:, :1], both[:, 1:2]
    adv_mean = jnp.sum(means, keepdims=True) / envs
    away = means - adv_mean
    adv_var = jnp.sum(spans + away * away, keepdims=True) / envs
    put(1, (advantage - adv_mean) * lax.rsqrt(adv_var + 1e-05))
    settle(gathered, shards - 1, send_sem)
    settle(joined, envs - 1, partial_sem)


def on_device(
    observations,
    stored_values,
    rewards,
    episode_ends,
    stale_list,
    discount_horizon,
    trace_horizon,
    bootstrap,
    norm_gain,
    input_weight,
    value_head,
):
    env_rows, steps, features = observations.shape
    slots = env_rows * steps // BLOCK
    width = input_weight.shape[1]
    lent_blocks = slots // 2
    blocks = observations.reshape(slots, BLOCK, features)
    in_space = pltpu.with_memory_space_constraint
    blocks = in_space(blocks, pltpu.HBM)
    listed = in_space(stale_list, pltpu.HBM)
    weight = in_space(input_weight, pltpu.HBM)
    vmem, smem, hbm = (
        pl.BlockSpec(memory_space=space) for space in (pltpu.VMEM, pltpu.SMEM, pltpu.HBM)
    )
    lent, their_list, held = pl.pallas_call(
        swap_kernel,
        name="swap",
        out_shape=(
            pltpu.VMEM((lent_blocks, BLOCK, features), observations.dtype),
            pltpu.HBM(stale_list.shape, stale_list.dtype),
            pltpu.VMEM(input_weight.shape, input_weight.dtype),
        ),
        in_specs=[hbm] * 3,
        out_specs=[vmem, hbm, vmem],
        scratch_shapes=[
            pltpu.SemaphoreType.DMA((lent_blocks + 1,)),
            pltpu.SemaphoreType.DMA((lent_blocks + 1,)),
            pltpu.SemaphoreType.DMA((4,)),
        ],
        compiler_params=pltpu.CompilerParams(
            collective_id=1, has_side_effects=True, vmem_limit_bytes=SWAP_LIMIT
        ),
    )(blocks, listed, weight)
    board = pl.pallas_call(
        critic_kernel,
        name="critic",
        out_shape=jax.ShapeDtypeStruct((4, ROWS, BLOCK), jnp.float32),
        in_specs=[smem] * 2 + [hbm] + [vmem] * 7,
        out_specs=vmem,
        scratch_shapes=[
            pltpu.VMEM((slots, BLOCK, features), jnp.bfloat16),
            pltpu.VMEM((2 * BLOCK, features), jnp.bfloat16),
            pltpu.VMEM((2 * BLOCK, features), jnp.bfloat16),
            pltpu.VMEM((1, features), jnp.float32),
            pltpu.VMEM((width // BLOCK, BLOCK), jnp.float32),
            pltpu.SMEM((2, ROWS), jnp.int32),
            pltpu.SMEM((2 * ROWS,), jnp.int32),
            pltpu.SemaphoreType.DMA((slots,)),
        ],
        compiler_params=pltpu.CompilerParams(vmem_limit_bytes=CRITIC_LIMIT),
    )(
        stale_list,
        in_space(their_list, pltpu.HBM),
        blocks,
        in_space(lent, pltpu.VMEM),
        in_space(held, pltpu.VMEM),
        stored_values,
        rewards,
        episode_ends,
        norm_gain.reshape(1, features),
        value_head.reshape(width // BLOCK, BLOCK),
    )
    envs, shards = lax.axis_size("env"), lax.axis_size("tm")
    joined = pl.pallas_call(
        functools.partial(exchange_kernel, shards),
        name="exchange",
        out_shape=jax.ShapeDtypeStruct((2, env_rows, steps), jnp.float32),
        in_specs=[smem] * 3 + [hbm],
        out_specs=vmem,
        scratch_shapes=[
            pltpu.VMEM((4, ROWS, BLOCK), jnp.float32),
            pltpu.VMEM((ROWS, BLOCK), jnp.float32),
            pltpu.VMEM((1, 1, BLOCK), jnp.float32),
            pltpu.VMEM((BLOCK, 1, BLOCK), jnp.float32),
            pltpu.VMEM((1, 1, BLOCK), jnp.float32),
            pltpu.VMEM((envs, 1, BLOCK), jnp.float32),
        ]
        + [pltpu.SemaphoreType.DMA] * 7,
        compiler_params=pltpu.CompilerParams(
            collective_id=0, has_side_effects=True, vmem_limit_bytes=EXCHANGE_LIMIT
        ),
    )(discount_horizon, trace_horizon, bootstrap, board)
    return joined[0], joined[1]


def solution(mesh):
    placed = (
        P("env", "tm", None),
        P("env", "tm"),
        P("env", "tm"),
        P("env", "tm"),
        P("env", "tm", None),
        P("env"),
        P("env"),
        P("env"),
        P(),
        P(),
        P(),
    )
    return jax.shard_map(
        on_device,
        mesh=mesh,
        in_specs=placed,
        out_specs=(P("env", "tm"), P("env", "tm")),
        check_vma=False,
    )
```

time: 59.7 us -> 57 us (0.955); the launches traced: 58.5 us -> 56.4 us
  local copies, waits for them, and re-layouts: 3.35 us -> 1.31 us
    pallas_call x1 -> x2, Pallas kernels: 34.6 us -> 21 us  [the longest x1 13.5 us: on_device(): pl.pallas_call(critic_kernel, name='critic', out_shape=jax.ShapeDtypeStru...]
    pallas_call x1, Pallas kernels: 20 us -> 33.5 us  [on_device(): pl.pallas_call(functools.partial(exchange_kernel, shards), name='exchange...]
    unnamed x8 -> x0, local copies, waits for them, and re-layouts: 2.75 us -> none
    squeeze x1, local copies, waits for them, and re-layouts: 0.6 us -> 1.31 us  [on_device(): return (joined[0], joined[1])]
where the time goes in v1:
time: 57 us; the launch traced here: 56.4 us
  Pallas kernels  54.5 us (96%)
  local copies, waits for them, and re-layouts  1.31 us (2%)
  between operations  0.65 us (1%)
    pallas_call x1, Pallas kernels, on_device(): pl.pallas_call(functools.partial(exchange_kernel, shards), name='exchange...  33.5 us
    pallas_call x1, Pallas kernels, on_device(): pl.pallas_call(critic_kernel, name='critic', out_shape=jax.ShapeDtypeStru...  13.5 us
    pallas_call x1, Pallas kernels, on_device(): pl.pallas_call(swap_kernel, name='swap', out_shape=(pltpu.VMEM((lent_bloc...  7.51 us
    squeeze x1, local copies, waits for them, and re-layouts, on_device(): return (joined[0], joined[1])  1.31 us

profile of v1, /device:TPU:1, one launch (start us, length us, event | category | flops | bytes accessed | tf_op | source)
XLA Modules:
  0.0 56.4 jit_solution(11014063343052386848)
XLA Ops:
  0.6 7.5 %swap.1 = (bf16[6,128,2048]{2,1,0:T(8,128)(2,1)S(1)}, s32[1,1,12]{2,1,0:T(1,128)}, bf16[2048,4096]{1,0:T(8,128)(2,1)S(1)}) custom-call(bf16[12,128,2048]{2,1,0:T(8,128)(2,1)} %bitcast.7, s32[1,1,12]{2,1,0:T(1,128)} %listed.3, bf16[2048,4096]{1,0:T(8,128)(2,1)} %weight.1), custom_call_target="tpu_custom_call" | custom-call | tf_op jit(solution)/shard_map/swap/pallas_call | solution.py:460
  8.1 13.5 %critic.1.board = f32[4,16,128]{2,1,0:T(8,128)} custom-call(s32[1,1,12]{2,1,0:T(1,128)} %listed.3, s32[1,1,12]{2,1,0:T(1,128)} %get-tuple-element.5.their_list, bf16[12,128,2048]{2,1,0:T(8,128)(2,1)} %bitcast.8, bf16[6,128,2048]{2,1,0:T(8,128)(2,1)S(1)} %get-tuple-element.6.lent, bf16[2048,4096]{1,0:T(8,128)(2,1)S(1)} %get-tuple-element.7.weight, ...), custom_call_target="tpu_custom_call" | custom-call | tf_op jit(solution)/shard_map/critic/pallas_call | solution.py:479
  21.6 33.5 %exchange.1 = f32[2,2,768]{2,1,0:T(2,128)} custom-call(f32[2]{0:T(128)} %discount_horizon.1, f32[2]{0:T(128)} %trace_horizon.1, f32[2]{0:T(128)} %bootstrap.1, f32[4,16,128]{2,1,0:T(8,128)} %critic.1.board), custom_call_target="tpu_custom_call" | custom-call | tf_op jit(solution)/shard_map/exchange/pallas_call | solution.py:509
  55.1 1.3 %slice_bitcast_fusion = (f32[2,768]{1,0:T(2,128)}, f32[2,768]{1,0:T(2,128)}) fusion(f32[2,2,768]{2,1,0:T(2,128)} %exchange.1), kind=kLoop, calls=%fused_computation | loop fusion | bytes 24576 | tf_op jit(solution)/shard_map/squeeze | solution.py:528

commit v2 on v0

--- a/solution.py
+++ b/solution.py
@@ -45,8 +45,7 @@
     message_ref,
     raw,
     held,
-    normed_a,
-    normed_b,
+    normed,
     fresh,
     packed,
     half_gain,
@@ -79,44 +78,43 @@
         def _():
             raw_copy(slot).start()
 
-    def wait_group(group):
-        for side in range(2):
-            slot = 2 * group + side
-
-            @pl.when(slot < count)
-            def _():
-                raw_copy(slot).wait()
-
-    def normalize(group, piece, target):
-        per_block = BLOCK // PIECE
-        slot = jnp.minimum(2 * group + piece // per_block, slots - 1)
-        rows = pl.ds((piece % per_block) * PIECE, PIECE)
-        widened = raw[slot, rows, :].astype(jnp.float32)
+    def wait_raw(slot):
+        @pl.when(slot < count)
+        def _():
+            raw_copy(slot).wait()
+
+    def normalize(start, length):
+        rows = pl.ds(start, length)
+        widened = raw[start // BLOCK, pl.ds(start % BLOCK, length), :].astype(jnp.float32)
         square_mean = jnp.mean(widened * widened, axis=-1, keepdims=True)
         scaled = widened * lax.rsqrt(square_mean + 1e-05) * half_gain[...]
-        target[pl.ds(piece * PIECE, PIECE), :] = scaled.astype(jnp.bfloat16)
-
-    def run_group(group, source, target, may_be_first):
-        pieces = 2 * BLOCK // PIECE
+        normed[rows, :] = scaled.astype(jnp.bfloat16)
+
+    def run_group(group, first):
+        rows = pl.ds(0, 2 * BLOCK)
+        if not first:
+            rows = pl.ds(pl.multiple_of(group * (2 * BLOCK), 2 * BLOCK), 2 * BLOCK)
         total = jnp.zeros((2 * BLOCK, BLOCK), jnp.float32)
+        ready = 2
         for c in range(chunks):
-            if may_be_first:
-
-                @pl.when(group == 0)
-                def _():
-                    held_copy(c).wait()
-
+            if first:
+                held_copy(c).wait()
+                bound = 2 + (c + 1) * (slots - 2) // chunks
+                for slot in range(ready, bound):
+                    wait_raw(slot)
             part = pl.ds(c * CHUNK, CHUNK)
             hidden = jnp.dot(
-                source[...], held[:, part], preferred_element_type=jnp.float32
+                normed[rows, :], held[:, part], preferred_element_type=jnp.float32
             )
             for k in range(CHUNK // BLOCK):
                 here = hidden[:, k * BLOCK : (k + 1) * BLOCK]
                 active = (here + here * jnp.tanh(here)).astype(jnp.bfloat16)
                 line = c * (CHUNK // BLOCK) + k
                 total += active.astype(jnp.float32) * head_rows[line : line + 1, :]
-            for piece in range(c * pieces // chunks, (c + 1) * pieces // chunks):
-                normalize(group + 1, piece, target)
+            if first:
+                for start in range(ready * BLOCK, bound * BLOCK, PIECE):
+                    normalize(start, PIECE)
+                ready = bound
         for side in range(2):
             slot = 2 * group + side
             scores = jnp.sum(
@@ -125,7 +123,19 @@
 
             @pl.when(slot < count)
             def _():
-                fresh[pl.ds(listed[0, 0, jnp.minimum(slot, slots - 1)], 1), :] = scores
+                fresh[pl.ds(listed[0, 0, slot], 1), :] = scores
+
+    @pl.when(count > 0)
+    def _():
+        for slot in range(2):
+            start_raw(slot)
+        after = 2
+        for c in range(chunks):
+            held_copy(c).start()
+            bound = 2 + (c + 1) * (slots - 2) // chunks
+            for slot in range(after, bound):
+                start_raw(slot)
+            after = bound
 
     for e in range(env_rows):
         for k in range(per_row):
@@ -136,33 +146,19 @@
 
     @pl.when(count > 0)
     def _():
-        for slot in range(2):
-            start_raw(slot)
-        for c in range(chunks):
-            held_copy(c).start()
-            if c == chunks // 2:
-                for slot in range(2, 4):
-                    start_raw(slot)
-        for slot in range(4, slots):
-            start_raw(slot)
         half_gain[...] = 0.5 * gain[...]
         head_rows[...] = head[...].astype(jnp.float32)
-        wait_group(0)
-        for piece in range(2 * BLOCK // PIECE):
-            normalize(0, piece, normed_a)
-
-        def two_groups(i, carry):
-            wait_group(2 * i + 1)
-            run_group(2 * i, normed_a, normed_b, True)
-
-            @pl.when(2 * i + 1 < groups)
-            def _():
-                wait_group(2 * i + 2)
-                run_group(2 * i + 1, normed_b, normed_a, False)
-
+        for slot in range(2):
+            wait_raw(slot)
+        for start in range(0, 2 * BLOCK, PIECE):
+            normalize(start, PIECE)
+        run_group(0, True)
+
+        def one_group(i, carry):
+            run_group(i, False)
             return carry
 
-        lax.fori_loop(0, (groups + 1) // 2, two_groups, 0)
+        lax.fori_loop(1, groups, one_group, 0)
 
     rows = fresh.shape[0]
     half = per_row
@@ -369,7 +365,8 @@
     env_rows, steps, features = observations.shape
     slots = env_rows * steps // BLOCK
     width = input_weight.shape[1]
-    shape = jax.ShapeDtypeStruct((env_rows, steps), jnp.float32)
+    shape = pltpu.VMEM((env_rows, steps), jnp.float32)
+    in_space = pltpu.with_memory_space_constraint
     vmem, smem, anywhere = (
         pl.BlockSpec(memory_space=pltpu.VMEM),
         pl.BlockSpec(memory_space=pltpu.SMEM),
@@ -378,14 +375,13 @@
     offset, factor, value, message = pl.pallas_call(
         sweep_kernel,
         name="sweep",
-        out_shape=(shape, shape, shape, jax.ShapeDtypeStruct((1, 1, BLOCK), jnp.float32)),
+        out_shape=(shape, shape, shape, pltpu.VMEM((1, 1, BLOCK), jnp.float32)),
         in_specs=[smem] * 4 + [anywhere] * 2 + [vmem] * 5,
         out_specs=[vmem] * 4,
         scratch_shapes=[
             pltpu.VMEM((slots, BLOCK, features), jnp.bfloat16),
             pltpu.VMEM((features, width), jnp.bfloat16),
-            pltpu.VMEM((2 * BLOCK, features), jnp.bfloat16),
-            pltpu.VMEM((2 * BLOCK, features), jnp.bfloat16),
+            pltpu.VMEM((slots * BLOCK, features), jnp.bfloat16),
             pltpu.VMEM((16, BLOCK), jnp.float32),
             pltpu.VMEM((2, 16, BLOCK), jnp.float32),
             pltpu.VMEM((1, features), jnp.float32),
@@ -393,14 +389,14 @@
             pltpu.SemaphoreType.DMA((slots,)),
             pltpu.SemaphoreType.DMA((width // CHUNK,)),
         ],
-        compiler_params=pltpu.CompilerParams(vmem_limit_bytes=59 * 1024 * 1024),
+        compiler_params=pltpu.CompilerParams(vmem_limit_bytes=57 * 1024 * 1024),
     )(
         stale_list,
         discount_horizon,
         trace_horizon,
         bootstrap,
-        observations.reshape(slots, BLOCK, features),
-        input_weight,
+        in_space(observations.reshape(slots, BLOCK, features), pltpu.HBM),
+        in_space(input_weight, pltpu.HBM),
         stored_values,
         rewards,
         episode_ends,
@@ -421,9 +417,9 @@
         ]
         + [pltpu.SemaphoreType.DMA] * 4,
         compiler_params=pltpu.CompilerParams(
-            collective_id=0, has_side_effects=True, vmem_limit_bytes=4 * 1024 * 1024
+            collective_id=0, has_side_effects=True, vmem_limit_bytes=57 * 1024 * 1024
         ),
-    )(message, offset, factor, value)
+    )(*(in_space(array, pltpu.VMEM) for array in (message, offset, factor, value)))
     return joined[0], joined[1]
 
 

time: 59.7 us -> 54.3 us (0.910); the launches traced: 58.5 us -> 54 us
  Pallas kernels: 54.5 us -> 52 us
  local copies, waits for them, and re-layouts: 3.35 us -> 1.31 us
    pallas_call x1, Pallas kernels: 34.6 us -> 21.1 us  [on_device(): pl.pallas_call(sweep_kernel, name='sweep', out_shape=(shape, shape, shape...]
    pallas_call x1, Pallas kernels: 20 us -> 30.9 us  [on_device(): pl.pallas_call(functools.partial(exchange_kernel, shards), name='exchange...]
    unnamed x8 -> x0, local copies, waits for them, and re-layouts: 2.75 us -> none
    squeeze x1, local copies, waits for them, and re-layouts: 0.6 us -> 1.31 us  [on_device(): return (joined[0], joined[1])]
where the time goes in v2:
time: 54.3 us; the launch traced here: 54 us
  Pallas kernels  52 us (96%)
  local copies, waits for them, and re-layouts  1.31 us (2%)
  between operations  0.65 us (1%)
    pallas_call x1, Pallas kernels, on_device(): pl.pallas_call(functools.partial(exchange_kernel, shards), name='exchange...  30.9 us
    pallas_call x1, Pallas kernels, on_device(): pl.pallas_call(sweep_kernel, name='sweep', out_shape=(shape, shape, shape...  21.1 us
    squeeze x1, local copies, waits for them, and re-layouts, on_device(): return (joined[0], joined[1])  1.31 us

profile of v2, /device:TPU:1, one launch (start us, length us, event | category | flops | bytes accessed | tf_op | source)
XLA Modules:
  0.0 54.0 jit_solution(16732578733431656622)
XLA Ops:
  0.6 21.1 %sweep.1 = (f32[2,768]{1,0:T(2,128)S(1)}, f32[2,768]{1,0:T(2,128)S(1)}, f32[2,768]{1,0:T(2,128)S(1)}, f32[1,1,128]{2,1,0:T(1,128)S(1)}) custom-call(s32[1,1,12]{2,1,0:T(1,128)} %listed.1, f32[2]{0:T(128)} %discount_horizon.1, f32[2]{0:T(128)} %trace_horizon.1, f32[2]{0:T(128)} %bootstrap.1, bf16[12,128,2048]{2,1,0:T(8,128)(2,1)} %bitcast.7, ...), custom_call_target="tpu_custom_call" | custom-call | tf_op jit(solution)/shard_map/sweep/pallas_call | solution.py:375
  21.8 30.9 %exchange.1 = f32[2,2,768]{2,1,0:T(2,128)} custom-call(f32[1,1,128]{2,1,0:T(1,128)S(1)} %get-tuple-element.6.message, f32[2,768]{1,0:T(2,128)S(1)} %get-tuple-element.7.offset_ref, f32[2,768]{1,0:T(2,128)S(1)} %get-tuple-element.8.factor_ref, f32[2,768]{1,0:T(2,128)S(1)} %get-tuple-element.9.value_ref), custom_call_target="tpu_custom_call" | custom-call | tf_op jit(solution)/shard_map/exchange/pallas_call | solution.py:407
  52.7 1.3 %slice_bitcast_fusion = (f32[2,768]{1,0:T(2,128)}, f32[2,768]{1,0:T(2,128)}) fusion(f32[2,2,768]{2,1,0:T(2,128)} %exchange.1), kind=kLoop, calls=%fused_computation | loop fusion | bytes 24576 | tf_op jit(solution)/shard_map/squeeze | solution.py:423

commit v3 on v2

--- a/solution.py
+++ b/solution.py
@@ -46,6 +46,7 @@
     raw,
     held,
     normed,
+    sums,
     fresh,
     packed,
     half_gain,
@@ -62,6 +63,8 @@
     for j in range(slots):
         count += (listed[0, 0, j] >= 0).astype(jnp.int32)
     groups = (count + 1) // 2
+    lead = (slots - chunks) // 2
+    spare = fresh.shape[0] - 1
 
     def raw_copy(slot):
         block = jnp.maximum(listed[0, 0, slot], 0)
@@ -83,59 +86,63 @@
         def _():
             raw_copy(slot).wait()
 
-    def normalize(start, length):
-        rows = pl.ds(start, length)
-        widened = raw[start // BLOCK, pl.ds(start % BLOCK, length), :].astype(jnp.float32)
+    def normalize(slot, piece):
+        source = raw[slot, pl.ds(piece * PIECE, PIECE), :]
+        widened = source.astype(jnp.float32)
         square_mean = jnp.mean(widened * widened, axis=-1, keepdims=True)
         scaled = widened * lax.rsqrt(square_mean + 1e-05) * half_gain[...]
-        normed[rows, :] = scaled.astype(jnp.bfloat16)
-
-    def run_group(group, first):
-        rows = pl.ds(0, 2 * BLOCK)
-        if not first:
-            rows = pl.ds(pl.multiple_of(group * (2 * BLOCK), 2 * BLOCK), 2 * BLOCK)
-        total = jnp.zeros((2 * BLOCK, BLOCK), jnp.float32)
-        ready = 2
-        for c in range(chunks):
-            if first:
-                held_copy(c).wait()
-                bound = 2 + (c + 1) * (slots - 2) // chunks
-                for slot in range(ready, bound):
-                    wait_raw(slot)
-            part = pl.ds(c * CHUNK, CHUNK)
-            hidden = jnp.dot(
-                normed[rows, :], held[:, part], preferred_element_type=jnp.float32
-            )
-            for k in range(CHUNK // BLOCK):
-                here = hidden[:, k * BLOCK : (k + 1) * BLOCK]
-                active = (here + here * jnp.tanh(here)).astype(jnp.bfloat16)
-                line = c * (CHUNK // BLOCK) + k
-                total += active.astype(jnp.float32) * head_rows[line : line + 1, :]
-            if first:
-                for start in range(ready * BLOCK, bound * BLOCK, PIECE):
-                    normalize(start, PIECE)
-                ready = bound
+        normed[slot, pl.ds(piece * PIECE, PIECE), :] = scaled.astype(jnp.bfloat16)
+
+    def normalize_block(slot):
+        for piece in range(BLOCK // PIECE):
+            normalize(slot, piece)
+
+    def scored(group, chunk, total):
+        rows = normed[pl.ds(2 * group, 2)].reshape(2 * BLOCK, features)
+        hidden = jnp.dot(
+            rows,
+            held[:, pl.ds(pl.multiple_of(chunk * CHUNK, CHUNK), CHUNK)],
+            preferred_element_type=jnp.float32,
+        )
+        for k in range(CHUNK // BLOCK):
+            here = hidden[:, k * BLOCK : (k + 1) * BLOCK]
+            active = (here + here * jnp.tanh(here)).astype(jnp.bfloat16)
+            line = pl.ds(chunk * (CHUNK // BLOCK) + k, 1)
+            total += active.astype(jnp.float32) * head_rows[line, :]
+        return total
+
+    def finish(group):
         for side in range(2):
             slot = 2 * group + side
-            scores = jnp.sum(
-                total[side * BLOCK : (side + 1) * BLOCK].T, axis=0, keepdims=True
-            )
-
-            @pl.when(slot < count)
-            def _():
-                fresh[pl.ds(listed[0, 0, slot], 1), :] = scores
+            scores = jnp.sum(sums[slot].T, axis=0, keepdims=True)
+            target = jnp.where(slot < count, listed[0, 0, slot], spare)
+            fresh[pl.ds(target, 1), :] = scores
+
+    def first_groups(c, carry):
+        held_copy(c).wait()
+        wait_raw(2 * lead + c)
+        for group in range(lead):
+            both = pl.ds(2 * group, 2)
+            before = sums[both].reshape(2 * BLOCK, BLOCK)
+            sums[both] = scored(group, c, before).reshape(2, BLOCK, BLOCK)
+        normalize_block(2 * lead + c)
+        return carry
+
+    def later_group(group, carry):
+        total = jnp.zeros((2 * BLOCK, BLOCK), jnp.float32)
+        finish(group - lead)
+        for c in range(chunks):
+            total = scored(group, c, total)
+        sums[pl.ds(2 * group, 2)] = total.reshape(2, BLOCK, BLOCK)
+        return carry
 
     @pl.when(count > 0)
     def _():
-        for slot in range(2):
+        for slot in range(2 * lead):
             start_raw(slot)
-        after = 2
         for c in range(chunks):
             held_copy(c).start()
-            bound = 2 + (c + 1) * (slots - 2) // chunks
-            for slot in range(after, bound):
-                start_raw(slot)
-            after = bound
+            start_raw(2 * lead + c)
 
     for e in range(env_rows):
         for k in range(per_row):
@@ -148,17 +155,14 @@
     def _():
         half_gain[...] = 0.5 * gain[...]
         head_rows[...] = head[...].astype(jnp.float32)
-        for slot in range(2):
+        sums[pl.ds(0, 2 * lead)] = jnp.zeros((2 * lead, BLOCK, BLOCK), jnp.float32)
+        for slot in range(2 * lead):
             wait_raw(slot)
-        for start in range(0, 2 * BLOCK, PIECE):
-            normalize(start, PIECE)
-        run_group(0, True)
-
-        def one_group(i, carry):
-            run_group(i, False)
-            return carry
-
-        lax.fori_loop(1, groups, one_group, 0)
+            normalize_block(slot)
+        lax.fori_loop(0, chunks, first_groups, 0)
+        lax.fori_loop(lead, groups, later_group, 0)
+        finish(jnp.maximum(groups - lead, 0))
+        finish(groups - 1)
 
     rows = fresh.shape[0]
     half = per_row
@@ -291,7 +295,6 @@
         part = target.at[pl.ds(0, length)]
         pltpu.make_async_copy(part, part, sem).wait()
 
-    gathered[...] = jnp.zeros_like(gathered)
     each_shard(greet)
     each_env(greet)
     pl.semaphore_wait(barrier, shards + envs - 2)
@@ -299,29 +302,27 @@
     gathered[pl.ds(tm, 1)] = message[...]
     settle(gathered, shards - 1, recv_sem)
 
-    fields = gathered[...].reshape(BLOCK, BLOCK).T
-    pair = lax.broadcasted_iota(jnp.int32, (8, BLOCK), 0)
-    lane = lax.broadcasted_iota(jnp.int32, (8, BLOCK), 1)
+    fields = gathered[...].reshape(shards, BLOCK)
+    shard = lax.broadcasted_iota(jnp.int32, (shards, BLOCK), 0)
+    lane = lax.broadcasted_iota(jnp.int32, (shards, BLOCK), 1)
 
     def field(k):
-        first = jnp.broadcast_to(fields[k : k + 1], (8, BLOCK))
-        second = jnp.broadcast_to(fields[FIELDS + k : FIELDS + k + 1], (8, BLOCK))
-        return jnp.where(pair == 0, first, second)
+        return shifted_left(fields, k) if k else fields
 
     offset, factor, last = field(0), field(1), field(3)
-    following = jnp.where(lane < shards - 1, shifted_left(field(2), 1), field(10))
+    following = jnp.where(shard < shards - 1, shifted_up(field(2), 1), field(10))
     jump = (following - last) * field(9)
     reached = offset + factor * jump
     by = 1
     while by < shards:
-        inside = lane + by < shards
-        reached = reached + factor * jnp.where(inside, shifted_left(reached, by), 0.0)
-        factor = factor * jnp.where(inside, shifted_left(factor, by), 1.0)
+        inside = shard + by < shards
+        reached = reached + factor * jnp.where(inside, shifted_up(reached, by), 0.0)
+        factor = factor * jnp.where(inside, shifted_up(factor, by), 1.0)
         by *= 2
-    entering = jump + jnp.where(lane < shards - 1, shifted_left(reached, 1), 0.0)
+    entering = jump + jnp.where(shard < shards - 1, shifted_up(reached, 1), 0.0)
     mean = field(4) + entering * field(5)
     inner = field(6) + entering * (2.0 * field(7) + entering * field(8))
-    counted = (pair < 2) & (lane < shards)
+    counted = (lane == 0) | (lane == FIELDS)
 
     def over_rows(array):
         return jnp.sum(jnp.where(counted, array, 0.0), keepdims=True) / (2 * shards)
@@ -332,8 +333,10 @@
     place = lax.broadcasted_iota(jnp.int32, (1, BLOCK), 1)
     line = jnp.where(place == 0, env_mean, jnp.where(place == 1, env_var, 0.0))
     partial[...] = line.reshape(partial.shape)
-    own = jnp.sum(jnp.where(lane == tm, entering, 0.0), axis=1, keepdims=True)
-    advantage = offset_ref[...] + factor_ref[...] * own[:2]
+    own = jnp.sum(jnp.where(shard == tm, entering, 0.0), axis=0, keepdims=True)
+    pair = lax.broadcasted_iota(jnp.int32, offset_ref.shape, 0)
+    own = jnp.where(pair == 0, own[:, :1], own[:, FIELDS : FIELDS + 1])
+    advantage = offset_ref[...] + factor_ref[...] * own
     result[0] = advantage + value_ref[...]
     each_env(send(partial, joined, env, partial_sem, joined_sem))
     joined[pl.ds(env, 1)] = partial[...]
@@ -381,7 +384,8 @@
         scratch_shapes=[
             pltpu.VMEM((slots, BLOCK, features), jnp.bfloat16),
             pltpu.VMEM((features, width), jnp.bfloat16),
-            pltpu.VMEM((slots * BLOCK, features), jnp.bfloat16),
+            pltpu.VMEM((slots, BLOCK, features), jnp.bfloat16),
+            pltpu.VMEM((slots, BLOCK, BLOCK), jnp.float32),
             pltpu.VMEM((16, BLOCK), jnp.float32),
             pltpu.VMEM((2, 16, BLOCK), jnp.float32),
             pltpu.VMEM((1, features), jnp.float32),
@@ -407,11 +411,11 @@
     joined = pl.pallas_call(
         functools.partial(exchange_kernel, shards),
         name="exchange",
-        out_shape=jax.ShapeDtypeStruct((2, env_rows, steps), jnp.float32),
+        out_shape=pltpu.VMEM((2, env_rows, steps), jnp.float32),
         in_specs=[vmem] * 4,
         out_specs=vmem,
         scratch_shapes=[
-            pltpu.VMEM((BLOCK, 1, BLOCK), jnp.float32),
+            pltpu.VMEM((shards, 1, BLOCK), jnp.float32),
             pltpu.VMEM((1, 1, BLOCK), jnp.float32),
             pltpu.VMEM((envs, 1, BLOCK), jnp.float32),
         ]

time: 54.3 us -> 52.4 us (0.965)
  Pallas kernels: 52 us -> 51 us
  local copies, waits for them, and re-layouts: 1.31 us -> 0.6 us
    pallas_call x1, Pallas kernels: 30.9 us -> 29.5 us  [on_device(): pl.pallas_call(functools.partial(exchange_kernel, shards), name='exchange...]
    squeeze x1, local copies, waits for them, and re-layouts: 1.31 us -> 0.6 us  [on_device(): return (joined[0], joined[1])]
where the time goes in v3:
time: 52.4 us; the launch traced here: 52.2 us
  Pallas kernels  51 us (97%)
  between operations  0.65 us (1%)
  local copies, waits for them, and re-layouts  0.6 us (1%)
    pallas_call x1, Pallas kernels, on_device(): pl.pallas_call(functools.partial(exchange_kernel, shards), name='exchange...  29.5 us
    pallas_call x1, Pallas kernels, on_device(): pl.pallas_call(sweep_kernel, name='sweep', out_shape=(shape, shape, shape...  21.5 us

profile of v3, /device:TPU:1, one launch (start us, length us, event | category | flops | bytes accessed | tf_op | source)
XLA Modules:
  0.0 52.2 jit_solution(11334495134795569068)
XLA Ops:
  0.6 21.5 %sweep.1 = (f32[2,768]{1,0:T(2,128)S(1)}, f32[2,768]{1,0:T(2,128)S(1)}, f32[2,768]{1,0:T(2,128)S(1)}, f32[1,1,128]{2,1,0:T(1,128)S(1)}) custom-call(s32[1,1,12]{2,1,0:T(1,128)} %listed.1, f32[2]{0:T(128)} %discount_horizon.1, f32[2]{0:T(128)} %trace_horizon.1, f32[2]{0:T(128)} %bootstrap.1, bf16[12,128,2048]{2,1,0:T(8,128)(2,1)} %bitcast.7, ...), custom_call_target="tpu_custom_call" | custom-call | tf_op jit(solution)/shard_map/sweep/pallas_call | solution.py:378
  22.1 29.5 %exchange.1 = f32[2,2,768]{2,1,0:T(2,128)S(1)} custom-call(f32[1,1,128]{2,1,0:T(1,128)S(1)} %get-tuple-element.6.message, f32[2,768]{1,0:T(2,128)S(1)} %get-tuple-element.7.offset_ref, f32[2,768]{1,0:T(2,128)S(1)} %get-tuple-element.8.factor_ref, f32[2,768]{1,0:T(2,128)S(1)} %get-tuple-element.9.value_ref), custom_call_target="tpu_custom_call" | custom-call | tf_op jit(solution)/shard_map/exchange/pallas_call | solution.py:411
  51.6 0.6 %slice_bitcast_fusion = (f32[2,768]{1,0:T(2,128)}, f32[2,768]{1,0:T(2,128)}) fusion(f32[2,2,768]{2,1,0:T(2,128)S(1)} %exchange.1), kind=kLoop, calls=%fused_computation | loop fusion | bytes 24576 | tf_op jit(solution)/shard_map/squeeze | solution.py:427

commit v4 on v3

--- a/solution.py
+++ b/solution.py
@@ -63,7 +63,6 @@
     for j in range(slots):
         count += (listed[0, 0, j] >= 0).astype(jnp.int32)
     groups = (count + 1) // 2
-    lead = (slots - chunks) // 2
     spare = fresh.shape[0] - 1
 
     def raw_copy(slot):
@@ -118,19 +117,23 @@
             target = jnp.where(slot < count, listed[0, 0, slot], spare)
             fresh[pl.ds(target, 1), :] = scores
 
+    def add_chunk(group, c):
+        both = pl.ds(2 * group, 2)
+        before = sums[both].reshape(2 * BLOCK, BLOCK)
+        sums[both] = scored(group, c, before).reshape(2, BLOCK, BLOCK)
+
     def first_groups(c, carry):
-        held_copy(c).wait()
-        wait_raw(2 * lead + c)
-        for group in range(lead):
-            both = pl.ds(2 * group, 2)
-            before = sums[both].reshape(2 * BLOCK, BLOCK)
-            sums[both] = scored(group, c, before).reshape(2, BLOCK, BLOCK)
-        normalize_block(2 * lead + c)
+        held_copy(c + 1).wait()
+        wait_raw(4 + c)
+        add_chunk(1, c)
+        add_chunk(0, c + 1)
+        normalize_block(4 + c)
         return carry
 
     def later_group(group, carry):
         total = jnp.zeros((2 * BLOCK, BLOCK), jnp.float32)
-        finish(group - lead)
+        finish(group - 2)
+        finish(group - 1)
         for c in range(chunks):
             total = scored(group, c, total)
         sums[pl.ds(2 * group, 2)] = total.reshape(2, BLOCK, BLOCK)
@@ -138,11 +141,15 @@
 
     @pl.when(count > 0)
     def _():
-        for slot in range(2 * lead):
+        for slot in range(2):
             start_raw(slot)
-        for c in range(chunks):
+        held_copy(0).start()
+        for slot in range(2, 4):
+            start_raw(slot)
+        for c in range(1, chunks):
             held_copy(c).start()
-            start_raw(2 * lead + c)
+            start_raw(3 + c)
+        start_raw(slots - 1)
 
     for e in range(env_rows):
         for k in range(per_row):
@@ -155,13 +162,26 @@
     def _():
         half_gain[...] = 0.5 * gain[...]
         head_rows[...] = head[...].astype(jnp.float32)
-        sums[pl.ds(0, 2 * lead)] = jnp.zeros((2 * lead, BLOCK, BLOCK), jnp.float32)
-        for slot in range(2 * lead):
+        sums[pl.ds(0, 4)] = jnp.zeros((4, BLOCK, BLOCK), jnp.float32)
+        for slot in range(2):
             wait_raw(slot)
             normalize_block(slot)
-        lax.fori_loop(0, chunks, first_groups, 0)
-        lax.fori_loop(lead, groups, later_group, 0)
-        finish(jnp.maximum(groups - lead, 0))
+        held_copy(0).wait()
+        for slot in range(2, 4):
+            wait_raw(slot)
+        add_chunk(0, 0)
+        for slot in range(2, 4):
+            normalize_block(slot)
+        lax.fori_loop(0, chunks - 1, first_groups, 0)
+        wait_raw(slots - 1)
+        add_chunk(1, chunks - 1)
+        normalize_block(slots - 1)
+        lax.fori_loop(2, groups, later_group, 0)
+
+        @pl.when(groups <= 2)
+        def _():
+            finish(0)
+
         finish(groups - 1)
 
     rows = fresh.shape[0]
@@ -213,18 +233,20 @@
         def mean_of(array):
             return jnp.sum(jnp.where(mine, array, 0.0), keepdims=True) / steps
 
-        mean_offset, mean_factor = mean_of(offset), mean_of(factor)
-        near, far = offset - mean_offset, factor - mean_factor
+        first_offset = row_offset[e * half : e * half + 1, :1]
+        first_factor = row_factor[e * half : e * half + 1, :1]
+        near, far = offset - first_offset, factor - first_factor
+        mean_near, mean_far = mean_of(near), mean_of(far)
         items = (
-            row_offset[e * half : e * half + 1, :1],
-            row_factor[e * half : e * half + 1, :1],
+            first_offset,
+            first_factor,
             value[e * half : e * half + 1, :1],
             value[(e + 1) * half - 1 : (e + 1) * half, BLOCK - 1 :],
-            mean_offset,
-            mean_factor,
-            mean_of(near * near),
-            mean_of(near * far),
-            mean_of(far * far),
+            first_offset + mean_near,
+            first_factor + mean_far,
+            mean_of(near * near) - mean_near * mean_near,
+            mean_of(near * far) - mean_near * mean_far,
+            mean_of(far * far) - mean_far * mean_far,
             1.0 / trace[e * half : e * half + 1, :1],
             jnp.full((1, 1), bootstrap[e], jnp.float32),
         )
@@ -258,20 +280,12 @@
     barrier = pltpu.get_barrier_semaphore()
 
     def each_shard(act):
-        def one(i, carry):
-            act(env, (tm + shards // 2 + i) % shards)
-            return carry
-
-        lax.fori_loop(0, shards // 2, one, 0)
-        lax.fori_loop(shards // 2 + 1, shards, one, 0)
+        for i in range(1, shards):
+            act(env, (tm + i * (shards // 2 + 1)) % shards)
 
     def each_env(act):
-        def one(i, carry):
-            act((env + envs // 2 + i) % envs, tm)
-            return carry
-
-        lax.fori_loop(0, envs // 2, one, 0)
-        lax.fori_loop(envs // 2 + 1, envs, one, 0)
+        for i in range(1, envs):
+            act((env + i * (envs // 2 + 1)) % envs, tm)
 
     def greet(to_env, to_tm):
         pl.semaphore_signal(

time: 52.4 us -> 52.4 us (level); the launches traced: 52.2 us -> 52.8 us
  Pallas kernels: 51 us -> 51.6 us
    pallas_call x1, Pallas kernels: 29.5 us -> 35.4 us  [on_device(): pl.pallas_call(functools.partial(exchange_kernel, shards), name='exchange...]
    pallas_call x1, Pallas kernels: 21.5 us -> 16.2 us  [on_device(): pl.pallas_call(sweep_kernel, name='sweep', out_shape=(shape, shape, shape...]
where the time goes in v4:
time: 52.4 us; the launch traced here: 52.8 us
  Pallas kernels  51.6 us (98%)
  between operations  0.65 us (1%)
  local copies, waits for them, and re-layouts  0.6 us (1%)
    pallas_call x1, Pallas kernels, on_device(): pl.pallas_call(functools.partial(exchange_kernel, shards), name='exchange...  35.4 us
    pallas_call x1, Pallas kernels, on_device(): pl.pallas_call(sweep_kernel, name='sweep', out_shape=(shape, shape, shape...  16.2 us

profile of v4, /device:TPU:1, one launch (start us, length us, event | category | flops | bytes accessed | tf_op | source)
XLA Modules:
  0.0 52.8 jit_solution(12307826992787953220)
XLA Ops:
  0.6 16.2 %sweep.1 = (f32[2,768]{1,0:T(2,128)S(1)}, f32[2,768]{1,0:T(2,128)S(1)}, f32[2,768]{1,0:T(2,128)S(1)}, f32[1,1,128]{2,1,0:T(1,128)S(1)}) custom-call(s32[1,1,12]{2,1,0:T(1,128)} %listed.1, f32[2]{0:T(128)} %discount_horizon.1, f32[2]{0:T(128)} %trace_horizon.1, f32[2]{0:T(128)} %bootstrap.1, bf16[12,128,2048]{2,1,0:T(8,128)(2,1)} %bitcast.7, ...), custom_call_target="tpu_custom_call" | custom-call | tf_op jit(solution)/shard_map/sweep/pallas_call | solution.py:392
  16.8 35.4 %exchange.1 = f32[2,2,768]{2,1,0:T(2,128)S(1)} custom-call(f32[1,1,128]{2,1,0:T(1,128)S(1)} %get-tuple-element.6.message, f32[2,768]{1,0:T(2,128)S(1)} %get-tuple-element.7.offset_ref, f32[2,768]{1,0:T(2,128)S(1)} %get-tuple-element.8.factor_ref, f32[2,768]{1,0:T(2,128)S(1)} %get-tuple-element.9.value_ref), custom_call_target="tpu_custom_call" | custom-call | tf_op jit(solution)/shard_map/exchange/pallas_call | solution.py:425
  52.2 0.6 %slice_bitcast_fusion = (f32[2,768]{1,0:T(2,128)}, f32[2,768]{1,0:T(2,128)}) fusion(f32[2,2,768]{2,1,0:T(2,128)S(1)} %exchange.1), kind=kLoop, calls=%fused_computation | loop fusion | bytes 24576 | tf_op jit(solution)/shard_map/squeeze | solution.py:441

commit v5 on v4

--- a/solution.py
+++ b/solution.py
@@ -34,11 +34,11 @@
     bootstrap,
     obs,
     weight,
-    stored,
-    rewards,
-    ends,
-    gain,
-    head,
+    stored_in,
+    rewards_in,
+    ends_in,
+    gain_in,
+    head_in,
     offset_ref,
     factor_ref,
     value_ref,
@@ -51,9 +51,29 @@
     packed,
     half_gain,
     head_rows,
+    stored,
+    rewards,
+    ends,
+    gain,
+    head,
     raw_sem,
     held_sem,
+    small_sem,
 ):
+    loads = [
+        pltpu.make_async_copy(source, target, small_sem.at[k])
+        for k, (source, target) in enumerate(
+            (
+                (stored_in, stored),
+                (rewards_in, rewards),
+                (ends_in, ends),
+                (gain_in, gain),
+                (head_in, head),
+            )
+        )
+    ]
+    for load in loads:
+        load.start()
     slots, _, features = raw.shape
     width = held.shape[1]
     chunks = width // CHUNK
@@ -151,6 +171,8 @@
             start_raw(3 + c)
         start_raw(slots - 1)
 
+    for load in loads:
+        load.wait()
     for e in range(env_rows):
         for k in range(per_row):
             row, part = pl.ds(e * per_row + k, 1), pl.ds(k * BLOCK, BLOCK)
@@ -393,7 +415,7 @@
         sweep_kernel,
         name="sweep",
         out_shape=(shape, shape, shape, pltpu.VMEM((1, 1, BLOCK), jnp.float32)),
-        in_specs=[smem] * 4 + [anywhere] * 2 + [vmem] * 5,
+        in_specs=[smem] * 4 + [anywhere] * 7,
         out_specs=[vmem] * 4,
         scratch_shapes=[
             pltpu.VMEM((slots, BLOCK, features), jnp.bfloat16),
@@ -404,8 +426,14 @@
             pltpu.VMEM((2, 16, BLOCK), jnp.float32),
             pltpu.VMEM((1, features), jnp.float32),
             pltpu.VMEM((width // BLOCK, BLOCK), jnp.float32),
+            pltpu.VMEM((env_rows, steps), jnp.float32),
+            pltpu.VMEM((env_rows, steps), jnp.float32),
+            pltpu.VMEM((env_rows, steps), jnp.int32),
+            pltpu.VMEM((1, features), jnp.float32),
+            pltpu.VMEM((width // BLOCK, BLOCK), jnp.bfloat16),
             pltpu.SemaphoreType.DMA((slots,)),
             pltpu.SemaphoreType.DMA((width // CHUNK,)),
+            pltpu.SemaphoreType.DMA((5,)),
         ],
         compiler_params=pltpu.CompilerParams(vmem_limit_bytes=57 * 1024 * 1024),
     )(

time: 52.4 us -> 51.3 us (0.979)
  Pallas kernels: 51.6 us -> 50.6 us
    pallas_call x1, Pallas kernels: 35.4 us -> 34.4 us  [on_device(): pl.pallas_call(functools.partial(exchange_kernel, shards), name='exchange...]
where the time goes in v5:
time: 51.3 us; the launch traced here: 51.8 us
  Pallas kernels  50.6 us (99%)
  between operations  0.65 us (1%)
  local copies, waits for them, and re-layouts  0.6 us (1%)
    pallas_call x1, Pallas kernels, on_device(): pl.pallas_call(functools.partial(exchange_kernel, shards), name='exchange...  34.4 us
    pallas_call x1, Pallas kernels, on_device(): pl.pallas_call(sweep_kernel, name='sweep', out_shape=(shape, shape, shape...  16.1 us

profile of v5, /device:TPU:1, one launch (start us, length us, event | category | flops | bytes accessed | tf_op | source)
XLA Modules:
  0.0 51.8 jit_solution(17876899446632971157)
XLA Ops:
  0.6 16.1 %sweep.1 = (f32[2,768]{1,0:T(2,128)S(1)}, f32[2,768]{1,0:T(2,128)S(1)}, f32[2,768]{1,0:T(2,128)S(1)}, f32[1,1,128]{2,1,0:T(1,128)S(1)}) custom-call(s32[1,1,12]{2,1,0:T(1,128)} %listed.1, f32[2]{0:T(128)} %discount_horizon.1, f32[2]{0:T(128)} %trace_horizon.1, f32[2]{0:T(128)} %bootstrap.1, bf16[12,128,2048]{2,1,0:T(8,128)(2,1)} %bitcast.7, ...), custom_call_target="tpu_custom_call" | custom-call | tf_op jit(solution)/shard_map/sweep/pallas_call | solution.py:414
  16.8 34.4 %exchange.1 = f32[2,2,768]{2,1,0:T(2,128)S(1)} custom-call(f32[1,1,128]{2,1,0:T(1,128)S(1)} %get-tuple-element.6.message, f32[2,768]{1,0:T(2,128)S(1)} %get-tuple-element.7.offset_ref, f32[2,768]{1,0:T(2,128)S(1)} %get-tuple-element.8.factor_ref, f32[2,768]{1,0:T(2,128)S(1)} %get-tuple-element.9.value_ref), custom_call_target="tpu_custom_call" | custom-call | tf_op jit(solution)/shard_map/exchange/pallas_call | solution.py:453
  51.2 0.6 %slice_bitcast_fusion = (f32[2,768]{1,0:T(2,128)}, f32[2,768]{1,0:T(2,128)}) fusion(f32[2,2,768]{2,1,0:T(2,128)S(1)} %exchange.1), kind=kLoop, calls=%fused_computation | loop fusion | bytes 24576 | tf_op jit(solution)/shard_map/squeeze | solution.py:469
